TPU v7x, 32 devices: a whole 2x2x4 slice. The times are simulated.
32 devices in a mesh: rows: 8 (over z, y), rep: 4 (over x, core).
Axes of the slice: x: 2, y: 2, z: 4, core: 2. Of those that a mesh axis runs over, the one named last changes fastest.
Arguments:
- event_slots: int32 [32, 128], P(('rows', 'rep')), may hold values from 0 to 143, as said below
- fetch_rows: int32 [32, 16], P(('rows', 'rep')), may hold values from 0 to 255, as said below
- fetch_counts: int32 [32, 8], P(('rows', 'rep')), may hold values from 1 to 2, as said below
- hot_table: float32 [128, 512], replicated, may hold values from -6 to 6
- hot_accum: float32 [128], replicated, may hold values from 0.05 to 2
- cold_table: float32 [2048, 512], P('rows'), may hold values from -6 to 6
- cold_accum: float32 [2048], P('rows'), may hold values from 0.05 to 2
- ln_gain: float32 [512], replicated, may hold values from 0.1 to 1.9
- ln_bias: float32 [512], replicated, may hold values from -3 to 3
- w_in: bfloat16 [512, 2048], replicated, may hold values from -0.25 to 0.25
- w_out: bfloat16 [512, 512], replicated, may hold values from -0.25 to 0.25
- out_grad: bfloat16 [4096, 512], P(('rows', 'rep')), may hold values from -6 to 6
Outputs:
- new_hot_table: float32 [128, 512], replicated
- new_hot_accum: float32 [128], replicated
- new_cold_table: float32 [2048, 512], P('rows')
- new_cold_accum: float32 [2048], P('rows')
Inputs may be any that keep to these rules, and one draw needn't show every extreme that they name: `event_slots`: rows of the lookup buffer: the 128 hot rows, then 2 slots for each of the 8 owners; an event names slot k of owner j only if k is below that device's fetch_counts for j. `fetch_rows`: rows local to the owner's shard, distinct within one owner's 2 slots of one device; slots at or past the count are padding. `fetch_counts`: some owner is asked for 2 rows by every device.
All inputs are finite; a program needn't handle non-finite values.
Results may differ from a plain program's by a relative error of at most 0.0065.
Values sent between devices are 32-bit elements; how exact they have to be, the bound alone decides.
No kernel may reach another device: no remote copies, remote signals or barrier semaphores. Data moves between devices by JAX's collectives and lax.ppermute only.
A program may use at most 64 MiB of HBM per device.

v0:
```python
import jax
import jax.numpy as jnp
from jax import lax
from jax.sharding import PartitionSpec as P

HEAD = 128
STEP_RATE = 0.5


def hstu_layer(looked_up, ln_gain, ln_bias, w_in, w_out):
    seq_rows = looked_up.shape[0]
    inner = w_out.shape[0]
    n_heads = inner // HEAD
    row_mean = jnp.mean(looked_up, axis=1, keepdims=True)
    centered = looked_up - row_mean
    row_var = jnp.mean(centered * centered, axis=1, keepdims=True)
    normed = (centered * lax.rsqrt(row_var + 1e-05) * ln_gain + ln_bias).astype(jnp.bfloat16)
    projected = jax.nn.silu(jnp.dot(normed, w_in, preferred_element_type=jnp.float32)).astype(
        jnp.bfloat16
    )
    gates_u, values_v, queries, keys_k = jnp.split(projected, 4, axis=1)
    head_shape = (seq_rows, n_heads, HEAD)
    scores = jnp.einsum(
        "qhd,khd->hqk",
        queries.reshape(head_shape),
        keys_k.reshape(head_shape),
        preferred_element_type=jnp.float32,
    ) * HEAD ** (-0.5)
    causal = (
        lax.broadcasted_iota(jnp.int32, (seq_rows, seq_rows), 0)
        >= lax.broadcasted_iota(jnp.int32, (seq_rows, seq_rows), 1)
    ).astype(jnp.float32)
    attention = (jax.nn.silu(scores) * causal * (1.0 / seq_rows)).astype(jnp.bfloat16)
    mixed_val = jnp.einsum(
        "hqk,khd->qhd", attention, values_v.reshape(head_shape), preferred_element_type=jnp.float32
    ).reshape(seq_rows, inner)
    mixed_mean = jnp.mean(mixed_val, axis=1, keepdims=True)
    mixed_cent = mixed_val - mixed_mean
    mixed_var = jnp.mean(mixed_cent * mixed_cent, axis=1, keepdims=True)
    gated_val = (mixed_cent * lax.rsqrt(mixed_var + 1e-06) * gates_u.astype(jnp.float32)).astype(
        jnp.bfloat16
    )
    layer_out = looked_up + jnp.dot(gated_val, w_out, preferred_element_type=jnp.float32)
    return layer_out.astype(jnp.bfloat16)


def adagrad(table_rows, accum_rows, grad_rows):
    new_accum = accum_rows + jnp.mean(grad_rows * grad_rows, axis=1)
    return (table_rows - STEP_RATE * grad_rows * lax.rsqrt(new_accum)[:, None], new_accum)


def on_device(
    event_slots,
    fetch_rows,
    fetch_counts,
    hot_table,
    hot_accum,
    cold_table,
    cold_accum,
    ln_gain,
    ln_bias,
    w_in,
    w_out,
    out_grad,
):
    owner_count = lax.axis_size("rows")
    per_owner = fetch_rows.shape[1] // owner_count
    hot_rows, feature_width = hot_table.shape
    rows_shard = cold_table.shape[0]
    wanted_rows = fetch_rows.reshape(owner_count, per_owner)
    live_mask = (
        lax.broadcasted_iota(jnp.int32, (owner_count, per_owner), 1)
        < fetch_counts.reshape(owner_count, 1)
    ).astype(jnp.float32)[:, :, None]
    asked_rows = lax.all_to_all(wanted_rows, "rows", split_axis=0, concat_axis=0, tiled=True)
    found = cold_table[asked_rows]
    fetched = lax.all_to_all(found, "rows", split_axis=0, concat_axis=0, tiled=True)
    buffer = jnp.concatenate(
        [hot_table, (fetched * live_mask).reshape(owner_count * per_owner, feature_width)], axis=0
    )
    event_rows = event_slots.reshape(-1)
    looked_up = buffer[event_rows]

    def forward(lookup_rows):
        return hstu_layer(lookup_rows, ln_gain, ln_bias, w_in, w_out)

    _, backward = jax.vjp(forward, looked_up)
    (d_lookup,) = backward(out_grad)
    buffer_grad = jax.ops.segment_sum(
        d_lookup, event_rows, num_segments=hot_rows + owner_count * per_owner
    )
    returned = buffer_grad[hot_rows:].reshape(owner_count, per_owner, feature_width) * live_mask
    arrived = lax.all_to_all(returned, "rows", split_axis=0, concat_axis=0, tiled=True)
    cold_grad = jax.ops.segment_sum(
        arrived.reshape(-1, feature_width), asked_rows.reshape(-1), num_segments=rows_shard
    )
    hot_grad = buffer_grad[:hot_rows]
    group_sum = lax.psum(hot_grad, "rep")
    my_share = lax.psum_scatter(group_sum, "rows", scatter_dimension=0, tiled=True)
    span_rows = my_share.shape[0]
    first_row = lax.axis_index("rows") * span_rows
    own_rows = lax.dynamic_slice_in_dim(hot_table, first_row, span_rows, 0)
    own_accum = lax.dynamic_slice_in_dim(hot_accum, first_row, span_rows, 0)
    part_rows, part_accum = adagrad(own_rows, own_accum, my_share)
    new_hot_table, new_hot_accum = (
        lax.all_gather(part_rows, "rows", axis=0, tiled=True),
        lax.all_gather(part_accum, "rows", axis=0, tiled=True),
    )
    summed_cold = lax.psum(cold_grad, "rep")
    new_cold_table, new_cold_accum = adagrad(cold_table, cold_accum, summed_cold)
    return (new_hot_table, new_hot_accum, new_cold_table, new_cold_accum)


def solution(mesh):
    return jax.shard_map(
        on_device,
        mesh=mesh,
        in_specs=(
            P(("rows", "rep"), None),
            P(("rows", "rep"), None),
            P(("rows", "rep"), None),
            P(),
            P(),
            P("rows", None),
            P("rows"),
            P(),
            P(),
            P(),
            P(),
            P(("rows", "rep"), None),
        ),
        out_specs=(P(), P(), P("rows", None), P("rows")),
        check_vma=False,
    )
```

profile of v0, /device:TPU:0, one launch (start us, length us, event | category | flops | bytes accessed | tf_op | source)
XLA Modules:
  0.0 198.6 jit_solution(12410957981415220685)
XLA Ops:
  8.0 0.5 broadcast.203
  8.5 1.4 reduce.10
  10.0 0.7 all_to_all.14
  10.6 7.3 %all-to-all-start = ((s32[8,1,2]{2,1,0:T(1,128)}), s32[8,1,2]{2,1,0:T(1,128)S(1)}, u32[]{:S(2)}, u32[]{:S(2)}) async-start(s32[8,1,2]{2,1,0:T(1,128)} %bitcast.1), calls=%async_computation | async-start | bytes 8192 | tf_op jit(solution)/shard_map/all_to_all | solution.py:75
  18.0 0.7 fusion.45
  18.6 0.7 fusion.44
  19.4 0.6 fusion.42
  20.0 4.4 %all-to-all-done = s32[8,1,2]{2,1,0:T(1,128)S(1)} async-done(((s32[8,1,2]{2,1,0:T(1,128)}), s32[8,1,2]{2,1,0:T(1,128)S(1)}, u32[]{:S(2)}, u32[]{:S(2)}) %all-to-all-start) | async-done | bytes 96 | tf_op jit(solution)/shard_map/all_to_all | solution.py:75
  24.6 1.6 gather_fusion
  26.3 0.6 reshape.204
  26.9 3.3 %all-to-all-start.1 = ((f32[8,2,512]{2,1,0:T(2,128)}), f32[8,2,512]{2,1,0:T(2,128)S(1)}, u32[]{:S(2)}, u32[]{:S(2)}) async-start(f32[8,2,512]{2,1,0:T(2,128)} %reshape.204), calls=%async_computation.1 | async-start | bytes 65536 | tf_op jit(solution)/shard_map/all_to_all | solution.py:77
  30.3 6.6 %all-to-all-done.1 = f32[8,2,512]{2,1,0:T(2,128)S(1)} async-done(((f32[8,2,512]{2,1,0:T(2,128)}), f32[8,2,512]{2,1,0:T(2,128)S(1)}, u32[]{:S(2)}, u32[]{:S(2)}) %all-to-all-start.1) | async-done | bytes 32800 | tf_op jit(solution)/shard_map/all_to_all | solution.py:77
  37.0 1.0 pad_maximum_fusion
  38.0 0.8 gather_fusion.1
  38.8 0.2 multiply_reduce_fusion.3
  39.1 1.5 multiply_convert_fusion
  40.6 0.8 copy-done.2
  41.6 0.2 convolution_multiply_fusion
  41.9 0.3 fusion.53
  42.3 0.3 copy-done.4
  42.6 0.1 copy.60
  42.8 1.5 multiply_reduce_fusion.2
  44.3 1.7 fusion.52
  46.0 0.3 convolution_convert_fusion.3
  46.4 0.3 fusion.19
  46.6 0.2 fusion.54
  46.8 0.2 fusion.55
  47.4 2.2 %multiply_reduce_fusion.1 = (f32[128]{0:T(128)S(1)}, f32[128,512]{1,0:T(8,128)S(1)}) fusion(f32[128,512]{1,0:T(8,128)S(1)} %gather_fusion.1, f32[128]{0:T(128)S(1)} %broadcast_multiply_fusion.3, f32[512]{0:T(512)S(1)} %copy-done.12, bf16[512,2048]{1,0:T(8,128)(2,1)S(1)} %copy-done, f32[128,2048]{1,0:T(8,128)} %get-tuple-element.19, ...), kind=kOutput, calls=%fused_computation.49 | convolution fusion | flops 273284992 | bytes 4197376 | tf_op jit(solution)/shard_map/transpose(jvp())/dot_general | solution.py:18
  49.7 0.2 fusion.51
  49.9 1.6 scatter_custom_fusion
  51.5 0.7 broadcast_multiply_fusion
  52.2 3.5 %all-to-all-start.2 = ((f32[8,2,512]{2,1,0:T(2,128)}), f32[8,2,512]{2,1,0:T(2,128)S(1)}, u32[]{:S(2)}, u32[]{:S(2)}) async-start(f32[8,2,512]{2,1,0:T(2,128)} %broadcast_multiply_fusion), calls=%async_computation.2 | async-start | bytes 65536 | tf_op jit(solution)/shard_map/all_to_all | solution.py:93
  55.8 0.7 reduce.11
  56.5 5.8 %all-to-all-done.2 = f32[8,2,512]{2,1,0:T(2,128)S(1)} async-done(((f32[8,2,512]{2,1,0:T(2,128)}), f32[8,2,512]{2,1,0:T(2,128)S(1)}, u32[]{:S(2)}, u32[]{:S(2)}) %all-to-all-start.2) | async-done | bytes 32800 | tf_op jit(solution)/shard_map/all_to_all | solution.py:93
  62.4 1.5 scatter_custom_fusion.1
  63.9 0.6 dynamic-slice
  65.2 0.7 slice.12
  65.9 28.9 %all-reduce.3.cloned.1.call-done = f32[256,512]{1,0:T(8,128)} async-done(((f32[256,512]{1,0:T(8,128)}), f32[256,512]{1,0:T(8,128)}) %all-reduce.3.cloned.1.call-update) | async-done | bytes 524304 | tf_op jit(solution)/shard_map/psum | solution.py:109
  94.8 1.2 multiply_reduce_fusion
  95.9 0.6 rsqrt_multiply_fusion
  96.5 1.9 multiply_subtract_fusion
  98.5 29.3 %reduce-scatter.2.cloned.1.call-done = f32[16,512]{1,0:T(8,128)} async-done(((f32[128,512]{1,0:T(8,128)}), f32[16,512]{1,0:T(8,128)}) %reduce-scatter.2.cloned.1.call-update) | async-done | bytes 32784 | tf_op jit(solution)/shard_map/reduce_scatter | solution.py:99
  127.7 10.8 %psum.16 = f32[16,512]{1,0:T(8,128)S(1)} all-reduce(f32[16,512]{1,0:T(8,128)} %reduce-scatter.2.cloned.1.call-done), channel_id=1, replica_groups=mesh['rows'=8,'rep'=4] {'rep'}, use_global_device_ids=true, to_apply=%region_9.10 | all-reduce | flops 8192 | bytes 65536 | tf_op jit(solution)/shard_map/psum | solution.py:98
  138.7 0.2 fusion.50
  138.8 0.8 multiply_subtract_fusion.1
  139.7 19.9 %all-reduce = f32[128]{0:T(128)} all-reduce(f32[128]{0:T(128)S(1)} %get-tuple-element.14), channel_id=1, replica_groups=mesh['rows'=8,'rep'=4] {'rows'}, use_global_device_ids=true, to_apply=%add | all-reduce | flops 128 | bytes 1024
  159.6 30.8 %all_gather.6 = f32[128,512]{1,0:T(8,128)S(1)} all-gather(f32[16,512]{1,0:T(8,128)S(1)} %multiply_subtract_fusion.1), channel_id=1, replica_groups=mesh['rows'=8,'rep'=4] {'rows'}, dimensions={0}, use_global_device_ids=true | all-gather | bytes 294912 | tf_op jit(solution)/shard_map/all_gather | solution.py:106
  190.4 0.7 copy.91
  (60 shorter events, 1.7 us)
Async XLA Ops:
  8.0 31.0 %copy-start = (bf16[512,2048]{1,0:T(8,128)(2,1)S(1)}, bf16[512,2048]{1,0:T(8,128)(2,1)}, u32[]{:S(2)}) copy-start(bf16[512,2048]{1,0:T(8,128)(2,1)} %param.21) | copy-start | bytes 6291460
  10.6 13.7 %all-to-all-start = ((s32[8,1,2]{2,1,0:T(1,128)}), s32[8,1,2]{2,1,0:T(1,128)S(1)}, u32[]{:S(2)}, u32[]{:S(2)}) async-start(s32[8,1,2]{2,1,0:T(1,128)} %bitcast.1), calls=%async_computation | async-start | bytes 8192 | tf_op jit(solution)/shard_map/all_to_all | solution.py:75
  17.9 21.1 %copy-start.11 = (f32[512]{0:T(512)S(1)}, f32[512]{0:T(512)}, u32[]{:S(2)}) copy-start(f32[512]{0:T(512)} %param.20) | copy-start | bytes 6148
  17.9 21.1 %copy-start.12 = (f32[512]{0:T(512)S(1)}, f32[512]{0:T(512)}, u32[]{:S(2)}) copy-start(f32[512]{0:T(512)} %param.19) | copy-start | bytes 6148
  26.9 10.0 %all-to-all-start.1 = ((f32[8,2,512]{2,1,0:T(2,128)}), f32[8,2,512]{2,1,0:T(2,128)S(1)}, u32[]{:S(2)}, u32[]{:S(2)}) async-start(f32[8,2,512]{2,1,0:T(2,128)} %reshape.204), calls=%async_computation.1 | async-start | bytes 65536 | tf_op jit(solution)/shard_map/all_to_all | solution.py:77
  40.6 0.8 copy-start.2
  40.6 2.1 %copy-start.3 = (bf16[128,512]{1,0:T(8,128)(2,1)S(1)}, bf16[128,512]{1,0:T(8,128)(2,1)}, u32[]{:S(2)}) copy-start(bf16[128,512]{1,0:T(8,128)(2,1)} %param.23) | copy-start | bytes 393220
  41.4 2.9 %copy-start.6 = (bf16[16,4,8,128]{3,2,1,0:T(8,128)(2,1)}, bf16[16,4,8,128]{3,2,1,0:T(8,128)(2,1)S(1)}, u32[]{:S(2)}) copy-start(bf16[16,4,8,128]{3,2,1,0:T(8,128)(2,1)S(1)} %get-tuple-element.11) | copy-start | bytes 393220
  41.9 0.7 copy-start.4
  42.7 3.3 %copy-start.5 = (f32[4,128,128]{2,1,0:T(8,128)S(1)}, f32[4,128,128]{2,1,0:T(8,128)}, u32[]{:S(2)}) copy-start(f32[4,128,128]{2,1,0:T(8,128)} %copy-done.4) | copy-start | bytes 786436
  42.7 3.6 %copy-start.8 = (f32[128,128]{1,0:T(8,128)S(1)}, f32[128,128]{1,0:T(8,128)}, u32[]{:S(2)}) copy-start(f32[128,128]{1,0:T(8,128)} %fusion.42) | copy-start | bytes 196612
  44.3 2.1 %copy-start.7 = (bf16[16,4,8,128]{3,2,1,0:T(8,128)(2,1)S(1)}, bf16[16,4,8,128]{3,2,1,0:T(8,128)(2,1)}, u32[]{:S(2)}) copy-start(bf16[16,4,8,128]{3,2,1,0:T(8,128)(2,1)} %copy-done.6) | copy-start | bytes 393220
  49.6 14.3 %copy-start.13 = (u32[32]{0:T(128)S(1)}, u32[32]{0:T(128)}, u32[]{:S(2)}) copy-start(u32[32]{0:T(128)} %constant.60) | copy-start | bytes 388
  49.6 46.3 %copy-start.9 = (f32[256]{0:T(256)S(1)}, f32[256]{0:T(256)}, u32[]{:S(2)}) copy-start(f32[256]{0:T(256)} %param.18) | copy-start | bytes 3076
  49.6 46.9 %copy-start.1 = (f32[256,512]{1,0:T(8,128)S(1)}, f32[256,512]{1,0:T(8,128)}, u32[]{:S(2)}) copy-start(f32[256,512]{1,0:T(8,128)} %param.17) | copy-start | bytes 1572868
  52.2 86.4 %copy-start.10 = (f32[128]{0:T(128)S(1)}, f32[128]{0:T(128)}, u32[]{:S(2)}) copy-start(f32[128]{0:T(128)} %param.16) | copy-start | bytes 1540
  52.2 10.1 %all-to-all-start.2 = ((f32[8,2,512]{2,1,0:T(2,128)}), f32[8,2,512]{2,1,0:T(2,128)S(1)}, u32[]{:S(2)}, u32[]{:S(2)}) async-start(f32[8,2,512]{2,1,0:T(2,128)} %broadcast_multiply_fusion), calls=%async_computation.2 | async-start | bytes 65536 | tf_op jit(solution)/shard_map/all_to_all | solution.py:93
  55.7 39.1 %all-reduce.3.cloned.1.call-start = ((), (), s32[]{:S(2)}) async-start(), calls=%async_computation.4 | async-start | bytes 1048576 | tf_op jit(solution)/shard_map/psum | solution.py:109
  63.9 63.9 %reduce-scatter.2.cloned.1.call-start = ((), (), s32[]{:S(2)}) async-start(), calls=%async_computation.5 | async-start | bytes 294912 | tf_op jit(solution)/shard_map/reduce_scatter | solution.py:99
Sparse Core Ops, SparseCore 0:
  64.0 30.7 all-reduce.2
Sparse Core Ops, SparseCore 1:
  68.2 59.4 reduce-scatter.1
where the time goes:
time: 199 us
  waiting for transfers between devices  75 us (38%)
  blocking collectives  61.5 us (31%)
  between operations  16.5 us (8%)
  other arithmetic  16.1 us (8%)
  starting transfers between devices  14.2 us (7%)
  local copies, waits for them, and re-layouts  8.5 us (4%)
  matrix products  6.7 us (3%)
    all_gather x1, blocking collectives, on_device(): lax.all_gather(part_rows, 'rows', axis=0, tiled=True)  30.8 us
    reduce_scatter x1, waiting for transfers between devices, on_device(): lax.psum_scatter(group_sum, 'rows', scatter_dimension=0, tiled=True)  29.3 us
    psum x1, waiting for transfers between devices, on_device(): summed_cold = lax.psum(cold_grad, 'rep')  28.9 us
    unnamed x1, blocking collectives  19.9 us
    psum x1, blocking collectives, on_device(): group_sum = lax.psum(hot_grad, 'rep')  10.8 us
    all_to_all x1, starting transfers between devices, on_device(): lax.all_to_all(wanted_rows, 'rows', split_axis=0, concat_axis=0, tiled=True)  7.31 us
    all_to_all x1, waiting for transfers between devices, on_device(): lax.all_to_all(found, 'rows', split_axis=0, concat_axis=0, tiled=True)  6.61 us
    all_to_all x1, waiting for transfers between devices, on_device(): lax.all_to_all(returned, 'rows', split_axis=0, concat_axis=0, tiled=True)  5.82 us
  transfers between devices with their start and end apart: 5, of which 5 were waited for; matrix products, arithmetic and copies ran while one was open for 4% of the time, Pallas kernels for 0%

commit v1 on v0

--- a/solution.py
+++ b/solution.py
@@ -106,7 +106,7 @@
         lax.all_gather(part_rows, "rows", axis=0, tiled=True),
         lax.all_gather(part_accum, "rows", axis=0, tiled=True),
     )
-    summed_cold = lax.psum(cold_grad, "rep")
+    summed_cold = jnp.sum(lax.all_gather(cold_grad, "rep"), axis=0)
     new_cold_table, new_cold_accum = adagrad(cold_table, cold_accum, summed_cold)
     return (new_hot_table, new_hot_accum, new_cold_table, new_cold_accum)
 

time: 199 us -> 187 us (0.940)
  waiting for transfers between devices: 75 us -> 62.9 us
    psum x1 -> x0, waiting for transfers between devices: 28.9 us -> none  [on_device(): summed_cold = lax.psum(cold_grad, 'rep')]
    reduce_scatter x1, waiting for transfers between devices: 29.3 us -> 46.1 us  [on_device(): lax.psum_scatter(group_sum, 'rows', scatter_dimension=0, tiled=True)]
  transfers between devices with their start and end apart: 5 -> 5, of which waited for: 5 -> 4; matrix products, arithmetic and copies ran while one was open for 4% -> 4% of each run, Pallas kernels for 0% -> 0%
where the time goes in v1:
time: 187 us; the launch traced here: 186 us
  waiting for transfers between devices  62.9 us (34%)
  blocking collectives  61.4 us (33%)
  between operations  16.6 us (9%)
  other arithmetic  16.5 us (9%)
  starting transfers between devices  14.1 us (8%)
  local copies, waits for them, and re-layouts  8.2 us (4%)
  matrix products  6.71 us (4%)
    reduce_scatter x1, waiting for transfers between devices, on_device(): lax.psum_scatter(group_sum, 'rows', scatter_dimension=0, tiled=True)  46.1 us
    all_gather x1, blocking collectives, on_device(): lax.all_gather(part_rows, 'rows', axis=0, tiled=True)  30.7 us
    unnamed x1, blocking collectives  19.9 us
    psum x1, blocking collectives, on_device(): group_sum = lax.psum(hot_grad, 'rep')  10.8 us
    all_to_all x1, starting transfers between devices, on_device(): lax.all_to_all(wanted_rows, 'rows', split_axis=0, concat_axis=0, tiled=True)  7.31 us
    all_to_all x1, waiting for transfers between devices, on_device(): lax.all_to_all(found, 'rows', split_axis=0, concat_axis=0, tiled=True)  6.56 us
    all_to_all x1, waiting for transfers between devices, on_device(): lax.all_to_all(returned, 'rows', split_axis=0, concat_axis=0, tiled=True)  5.82 us
    all_to_all x1, waiting for transfers between devices, on_device(): lax.all_to_all(wanted_rows, 'rows', split_axis=0, concat_axis=0, tiled=True)  4.34 us
  transfers between devices with their start and end apart: 5, of which 4 were waited for; matrix products, arithmetic and copies ran while one was open for 4% of the time, Pallas kernels for 0%

profile of v1, /device:TPU:0, one launch (start us, length us, event | category | flops | bytes accessed | tf_op | source)
XLA Modules:
  0.0 186.4 jit_solution(5275143175619925553)
XLA Ops:
  8.0 0.5 broadcast.203
  8.5 1.4 reduce.10
  10.0 0.7 all_to_all.14
  10.6 7.3 %all-to-all-start = ((s32[8,1,2]{2,1,0:T(1,128)}), s32[8,1,2]{2,1,0:T(1,128)S(1)}, u32[]{:S(2)}, u32[]{:S(2)}) async-start(s32[8,1,2]{2,1,0:T(1,128)} %bitcast.1), calls=%async_computation | async-start | bytes 8192 | tf_op jit(solution)/shard_map/all_to_all | solution.py:75
  18.0 0.7 fusion.45
  18.7 0.7 fusion.44
  19.4 0.6 fusion.42
  20.0 4.3 %all-to-all-done = s32[8,1,2]{2,1,0:T(1,128)S(1)} async-done(((s32[8,1,2]{2,1,0:T(1,128)}), s32[8,1,2]{2,1,0:T(1,128)S(1)}, u32[]{:S(2)}, u32[]{:S(2)}) %all-to-all-start) | async-done | bytes 96 | tf_op jit(solution)/shard_map/all_to_all | solution.py:75
  24.6 1.6 gather_fusion
  26.3 0.6 reshape.204
  26.9 3.3 %all-to-all-start.1 = ((f32[8,2,512]{2,1,0:T(2,128)}), f32[8,2,512]{2,1,0:T(2,128)S(1)}, u32[]{:S(2)}, u32[]{:S(2)}) async-start(f32[8,2,512]{2,1,0:T(2,128)} %reshape.204), calls=%async_computation.1 | async-start | bytes 65536 | tf_op jit(solution)/shard_map/all_to_all | solution.py:77
  30.3 6.6 %all-to-all-done.1 = f32[8,2,512]{2,1,0:T(2,128)S(1)} async-done(((f32[8,2,512]{2,1,0:T(2,128)}), f32[8,2,512]{2,1,0:T(2,128)S(1)}, u32[]{:S(2)}, u32[]{:S(2)}) %all-to-all-start.1) | async-done | bytes 32800 | tf_op jit(solution)/shard_map/all_to_all | solution.py:77
  37.0 1.0 pad_maximum_fusion
  38.0 0.8 gather_fusion.1
  38.8 0.2 multiply_reduce_fusion.3
  39.1 1.5 multiply_convert_fusion
  40.6 0.7 copy-done.2
  41.7 0.2 convolution_multiply_fusion
  41.9 0.3 fusion.53
  42.2 0.6 fusion.21
  42.8 0.1 copy.75
  43.0 1.5 multiply_reduce_fusion.2
  44.5 0.7 fusion.47
  45.2 1.1 fusion.52
  46.3 0.3 convolution_convert_fusion.3
  46.7 0.3 fusion.19
  46.9 0.2 fusion.54
  47.1 0.2 fusion.55
  47.7 2.2 %multiply_reduce_fusion.1 = (f32[128]{0:T(128)S(1)}, f32[128,512]{1,0:T(8,128)S(1)}) fusion(f32[128,512]{1,0:T(8,128)S(1)} %gather_fusion.1, f32[128]{0:T(128)S(1)} %broadcast_multiply_fusion.3, f32[512]{0:T(512)S(1)} %copy-done.17, bf16[512,2048]{1,0:T(8,128)(2,1)S(1)} %copy-done, f32[128,2048]{1,0:T(8,128)} %get-tuple-element.19, ...), kind=kOutput, calls=%fused_computation.49 | convolution fusion | flops 273284992 | bytes 4197376 | tf_op jit(solution)/shard_map/transpose(jvp())/dot_general | solution.py:18
  50.0 0.2 fusion.51
  50.2 1.6 scatter_custom_fusion
  51.8 0.7 slice.12
  52.6 0.7 broadcast_multiply_fusion
  53.3 3.3 %all-to-all-start.2 = ((f32[8,2,512]{2,1,0:T(2,128)}), f32[8,2,512]{2,1,0:T(2,128)S(1)}, u32[]{:S(2)}, u32[]{:S(2)}) async-start(f32[8,2,512]{2,1,0:T(2,128)} %broadcast_multiply_fusion), calls=%async_computation.2 | async-start | bytes 65536 | tf_op jit(solution)/shard_map/all_to_all | solution.py:93
  56.7 0.7 reduce.11
  57.5 5.8 %all-to-all-done.2 = f32[8,2,512]{2,1,0:T(2,128)S(1)} async-done(((f32[8,2,512]{2,1,0:T(2,128)}), f32[8,2,512]{2,1,0:T(2,128)S(1)}, u32[]{:S(2)}, u32[]{:S(2)}) %all-to-all-start.2) | async-done | bytes 32800 | tf_op jit(solution)/shard_map/all_to_all | solution.py:93
  63.3 1.5 scatter_custom_fusion.1
  64.8 0.6 dynamic-slice
  66.1 46.1 %reduce-scatter.2.cloned.1.call-done = f32[16,512]{1,0:T(8,128)} async-done(((f32[128,512]{1,0:T(8,128)}), f32[16,512]{1,0:T(8,128)}) %reduce-scatter.2.cloned.1.call-update) | async-done | bytes 32784 | tf_op jit(solution)/shard_map/reduce_scatter | solution.py:99
  112.2 10.8 %psum.8 = f32[16,512]{1,0:T(8,128)S(1)} all-reduce(f32[16,512]{1,0:T(8,128)} %reduce-scatter.2.cloned.1.call-done), channel_id=1, replica_groups=mesh['rows'=8,'rep'=4] {'rep'}, use_global_device_ids=true, to_apply=%region_9.10 | all-reduce | flops 8192 | bytes 65536 | tf_op jit(solution)/shard_map/psum | solution.py:98
  123.1 0.2 fusion.50
  123.3 0.8 multiply_subtract_fusion.1
  124.1 30.7 %all_gather.12 = f32[128,512]{1,0:T(8,128)S(1)} all-gather(f32[16,512]{1,0:T(8,128)S(1)} %multiply_subtract_fusion.1), channel_id=1, replica_groups=mesh['rows'=8,'rep'=4] {'rows'}, dimensions={0}, use_global_device_ids=true | all-gather | bytes 294912 | tf_op jit(solution)/shard_map/all_gather | solution.py:106
  154.9 19.9 %all-reduce = f32[128]{0:T(128)} all-reduce(f32[128]{0:T(128)S(1)} %get-tuple-element.14), channel_id=1, replica_groups=mesh['rows'=8,'rep'=4] {'rows'}, use_global_device_ids=true, to_apply=%add | all-reduce | flops 128 | bytes 1024
  174.8 1.9 %reduce_sum.124 = f32[256,512]{1,0:T(8,128)S(1)} reduce(f32[4,256,512]{2,1,0:T(8,128)} %bitcast.71, f32[]{:T(128)} %constant.21.clone.1), dimensions={0}, to_apply=%region_13.14 | reduce | flops 393216 | bytes 2621444 | tf_op jit(solution)/shard_map/reduce_sum | solution.py:109
  176.8 0.6 rsqrt_multiply_fusion
  177.3 0.9 multiply_subtract_fusion
  178.2 0.7 copy.105
  (71 shorter events, 1.7 us)
Async XLA Ops:
  8.0 31.1 %copy-start = (bf16[512,2048]{1,0:T(8,128)(2,1)S(1)}, bf16[512,2048]{1,0:T(8,128)(2,1)}, u32[]{:S(2)}) copy-start(bf16[512,2048]{1,0:T(8,128)(2,1)} %param.21) | copy-start | bytes 6291460
  10.6 13.7 %all-to-all-start = ((s32[8,1,2]{2,1,0:T(1,128)}), s32[8,1,2]{2,1,0:T(1,128)S(1)}, u32[]{:S(2)}, u32[]{:S(2)}) async-start(s32[8,1,2]{2,1,0:T(1,128)} %bitcast.1), calls=%async_computation | async-start | bytes 8192 | tf_op jit(solution)/shard_map/all_to_all | solution.py:75
  17.9 21.1 %copy-start.15 = (f32[512]{0:T(512)S(1)}, f32[512]{0:T(512)}, u32[]{:S(2)}) copy-start(f32[512]{0:T(512)} %param.20) | copy-start | bytes 6148
  17.9 21.1 %copy-start.16 = (f32[512]{0:T(512)S(1)}, f32[512]{0:T(512)}, u32[]{:S(2)}) copy-start(f32[512]{0:T(512)} %param.19) | copy-start | bytes 6148
  18.0 23.9 %copy-start.6 = (f32[128,128]{1,0:T(8,128)}, f32[128,128]{1,0:T(8,128)S(1)}, u32[]{:S(2)}) copy-start(f32[128,128]{1,0:T(8,128)S(1)} %fusion.43) | copy-start | bytes 196612
  26.9 10.0 %all-to-all-start.1 = ((f32[8,2,512]{2,1,0:T(2,128)}), f32[8,2,512]{2,1,0:T(2,128)S(1)}, u32[]{:S(2)}, u32[]{:S(2)}) async-start(f32[8,2,512]{2,1,0:T(2,128)} %reshape.204), calls=%async_computation.1 | async-start | bytes 65536 | tf_op jit(solution)/shard_map/all_to_all | solution.py:77
  30.2 81.9 %reduce-scatter.2.cloned.1.call-start = ((), (), s32[]{:S(2)}) async-start(), calls=%async_computation.5 | async-start | bytes 294912 | tf_op jit(solution)/shard_map/reduce_scatter | solution.py:99
  39.0 1.6 copy-start.12
  39.1 1.5 copy-start.10
  40.6 0.8 copy-start.2
  40.6 2.3 %copy-start.3 = (bf16[128,512]{1,0:T(8,128)(2,1)S(1)}, bf16[128,512]{1,0:T(8,128)(2,1)}, u32[]{:S(2)}) copy-start(bf16[128,512]{1,0:T(8,128)(2,1)} %param.23) | copy-start | bytes 393220
  41.4 1.4 copy-start.4
  42.9 3.4 %copy-start.7 = (f32[128,128]{1,0:T(8,128)S(1)}, f32[128,128]{1,0:T(8,128)}, u32[]{:S(2)}) copy-start(f32[128,128]{1,0:T(8,128)} %copy-done.6) | copy-start | bytes 196612
  43.0 3.7 %copy-start.5 = (bf16[16,4,8,128]{3,2,1,0:T(8,128)(2,1)S(1)}, bf16[16,4,8,128]{3,2,1,0:T(8,128)(2,1)}, u32[]{:S(2)}) copy-start(bf16[16,4,8,128]{3,2,1,0:T(8,128)(2,1)} %copy-done.4) | copy-start | bytes 393220
  43.0 3.7 %copy-start.8 = (f32[128,128]{1,0:T(8,128)S(1)}, f32[128,128]{1,0:T(8,128)}, u32[]{:S(2)}) copy-start(f32[128,128]{1,0:T(8,128)} %fusion.42) | copy-start | bytes 196612
  46.6 1.1 copy-start.17
  47.7 2.2 %copy-start.13 = (f32[128]{0:T(128)S(1)}, f32[128]{0:T(128)}, u32[]{:S(2)}) copy-start(f32[128]{0:T(128)} %copy-done.12) | copy-start | bytes 1540
  47.7 2.3 %copy-start.11 = (f32[128]{0:T(128)S(1)}, f32[128]{0:T(128)}, u32[]{:S(2)}) copy-start(f32[128]{0:T(128)} %copy-done.10) | copy-start | bytes 1540
  49.9 14.9 %copy-start.18 = (u32[32]{0:T(128)S(1)}, u32[32]{0:T(128)}, u32[]{:S(2)}) copy-start(u32[32]{0:T(128)} %constant.60) | copy-start | bytes 388
  49.9 73.2 %copy-start.14 = (f32[128]{0:T(128)S(1)}, f32[128]{0:T(128)}, u32[]{:S(2)}) copy-start(f32[128]{0:T(128)} %param.16) | copy-start | bytes 1540
  53.3 10.0 %all-to-all-start.2 = ((f32[8,2,512]{2,1,0:T(2,128)}), f32[8,2,512]{2,1,0:T(2,128)S(1)}, u32[]{:S(2)}, u32[]{:S(2)}) async-start(f32[8,2,512]{2,1,0:T(2,128)} %broadcast_multiply_fusion), calls=%async_computation.2 | async-start | bytes 65536 | tf_op jit(solution)/shard_map/all_to_all | solution.py:93
  56.7 118.1 %all-gather.3.cloned.1.call-start = ((), (), s32[]{:S(2)}) async-start(), calls=%async_computation.4 | async-start | bytes 2621440 | tf_op jit(solution)/shard_map/all_gather | solution.py:109
  64.8 112.0 %copy-start.9 = (f32[256]{0:T(256)S(1)}, f32[256]{0:T(256)}, u32[]{:S(2)}) copy-start(f32[256]{0:T(256)} %param.18) | copy-start | bytes 3076
  64.8 112.6 %copy-start.1 = (f32[256,512]{1,0:T(8,128)S(1)}, f32[256,512]{1,0:T(8,128)}, u32[]{:S(2)}) copy-start(f32[256,512]{1,0:T(8,128)} %param.17) | copy-start | bytes 1572868
Sparse Core Ops, SparseCore 0:
  52.7 59.4 reduce-scatter.1
Sparse Core Ops, SparseCore 1:
  64.9 19.7 all-gather.2
